TPU v7x, 32 devices: a whole 2x2x4 slice. The times are simulated.
32 devices in a mesh: dp: 4 (over y, core), slab: 8 (over z, x).
Axes of the slice: x: 2, y: 2, z: 4, core: 2. Of those that a mesh axis runs over, the one named last changes fastest.
Arguments:
- acts: bfloat16 [4, 32, 8, 128, 128], P('dp', None, 'slab'), may hold values from -24 to 24
- grads: bfloat16 [4, 32, 8, 128, 128], P('dp', None, 'slab'), may hold values from -6 to 6
- picks: int32 [4, 4096], P('dp', 'slab'), may hold values from 0 to 31
Outputs:
- weight_grad: float32 [32, 864], replicated
- update: float32 [32, 864], replicated
Inputs may be any that keep to these rules, and one draw needn't show every extreme that they name: `picks`: one cell is sampled in each aligned block of 32 of a device's cells, counted plane by plane, row by row, column by column; entry e of a device's 512 entries belongs to block e.
All inputs are finite; a program needn't handle non-finite values.
Results may differ from a plain program's by a relative error of at most 0.0003.
Values may be sent and summed in bfloat16 or wider, within the bound.
A program may use at most 128 MiB of HBM per device.

v0:
```python
import math

import jax
import jax.numpy as jnp
from jax import lax
from jax.sharding import PartitionSpec as P

epsilon = 1e-06
damping = 0.1
trust_region_limit = 0.3
learning_rate = 0.01


def padded_2(shard, sides, width):
    for axis, dim in sides:
        size, length = (lax.axis_size(axis), shard.shape[dim])
        up = [(i, (i + 1) % size) for i in range(size - 1)]
        down = [(j, i) for i, j in up]
        last = lax.slice_in_dim(shard, length - width, length, axis=dim)
        leading = lax.slice_in_dim(shard, 0, width, axis=dim)
        before = lax.ppermute(last, axis, up)
        after = lax.ppermute(leading, axis, down)
        shard = jnp.concatenate([before, shard, after], axis=dim)
    return shard


def cholesky_apply(factor, values):
    halfway = lax.linalg.triangular_solve(factor, values, left_side=True, lower=True)
    return lax.linalg.triangular_solve(
        factor, halfway, left_side=True, lower=True, transpose_a=True
    )


def take_columns(matrix, indices):
    return jnp.take(matrix, indices, axis=1)


def shards(acts, grads, picks):
    volumes, channels, planes, height, kernel_extent = acts.shape
    outputs = grads.shape[1]
    sample_count = picks.shape[1]
    plane_size = (height + 2) * (kernel_extent + 2)
    shifts = jnp.array(
        [
            along_z * plane_size + along_y * (kernel_extent + 2) + along_x
            for along_z in range(3)
            for along_y in range(3)
            for along_x in range(3)
        ],
        dtype=jnp.int32,
    )
    extended = padded_2(acts, (("slab", 2),), 1)
    padded = jnp.pad(extended, ((0, 0), (0, 0), (0, 0), (1, 1), (1, 1)))
    grad_rows = grads.reshape(volumes, outputs, -1)
    products = []
    for offset in range(27):
        along_z, along_y, along_x = (offset // 9, offset // 3 % 3, offset % 3)
        shifted = padded[
            :,
            :,
            along_z : along_z + planes,
            along_y : along_y + height,
            along_x : along_x + kernel_extent,
        ].reshape(volumes, channels, -1)
        products.append(
            lax.dot_general(
                grad_rows, shifted, (((0, 2), (0, 2)), ((), ())), preferred_element_type=jnp.float32
            )
        )
    gradient_portion = jnp.concatenate(products, axis=1)
    sample_index = jnp.arange(sample_count, dtype=jnp.int32)
    position = sample_index[None, :] * 32 + picks
    plane_index = position // (height * kernel_extent)
    row_index = position // kernel_extent % height
    column_index = position % kernel_extent
    base_index = plane_index * plane_size + row_index * (kernel_extent + 2) + column_index
    flat_index = (shifts[None, :, None] + base_index[:, None, :]).reshape(volumes, -1)
    selected_values = jax.vmap(take_columns)(padded.reshape(volumes, channels, -1), flat_index)
    input_patches = selected_values.reshape(volumes, channels, 27, sample_count).transpose(
        0, 2, 1, 3
    )
    grad_samples = jax.vmap(take_columns)(grad_rows, position)
    gradient_gram_matrix = jnp.einsum(
        "vcs,vds->cd", grad_samples, grad_samples, preferred_element_type=jnp.float32
    )
    gram = jnp.einsum(
        "mfuh,mioh->fuio", input_patches, input_patches, preferred_element_type=jnp.float32
    ).reshape(27 * channels, 27 * channels)
    summed_acts, summed_grads, summed_weight = lax.psum(
        (gram, gradient_gram_matrix, gradient_portion), ("dp", "slab")
    )
    positions = (
        volumes * lax.axis_size("dp") * planes * lax.axis_size("slab") * height * kernel_extent
    )
    samples = volumes * lax.axis_size("dp") * sample_count * lax.axis_size("slab")
    weight_grad = summed_weight / math.sqrt(positions)
    factor_acts = summed_acts / samples
    factor_grads = summed_grads / samples
    patch_width = factor_acts.shape[0]
    trace_ratio = jnp.sqrt(
        (jnp.trace(factor_acts) / patch_width + epsilon)
        / (jnp.trace(factor_grads) / outputs + epsilon)
    )
    damped_activation_factor = factor_acts + trace_ratio * math.sqrt(damping) * jnp.eye(
        patch_width, dtype=jnp.float32
    )
    damped_grads = factor_grads + math.sqrt(damping) / trace_ratio * jnp.eye(
        outputs, dtype=jnp.float32
    )
    chol_acts = jnp.linalg.cholesky(damped_activation_factor)
    chol_grads = jnp.linalg.cholesky(damped_grads)
    left_solved = cholesky_apply(chol_grads, weight_grad)
    precond = cholesky_apply(chol_acts, left_solved.T).T
    quadratic = jnp.sum(precond * weight_grad)
    clip_factor = jnp.minimum(1.0, jnp.sqrt(trust_region_limit / (learning_rate**2 * quadratic)))
    return (weight_grad, clip_factor * precond)


def solution(mesh):
    return jax.shard_map(
        shards,
        mesh=mesh,
        in_specs=(
            P("dp", None, "slab", None, None),
            P("dp", None, "slab", None, None),
            P("dp", "slab"),
        ),
        out_specs=(P(), P()),
        check_vma=False,
    )
```

profile of v0, /device:TPU:0, one launch (start us, length us, event | category | flops | bytes accessed | tf_op | source)
XLA Modules:
  0.0 799.0 jit_solution(2452920314638502882)
XLA Ops:
  7.2 1.9 copy.40
  9.1 4.9 collective-permute-start
  18.2 2.8 convolution_bitcast_fusion.13
  21.0 37.8 %collective-permute-done = bf16[1,32,1,128,128]{4,1,3,2,0:T(8,128)(2,1)S(1)} collective-permute-done((bf16[1,32,1,128,128]{4,1,3,2,0:T(8,128)(2,1)S(1)}, bf16[1,32,1,128,128]{4,1,3,2,0:T(8,128)(2,1)S(1)}, u32[]{:S(2)}, u32[]{:S(2)}) %collective-permute-start) | collective-permute-done | bytes 1048608 | tf_op jit(solution)/shard_map/ppermute | solution.py:21
  58.9 7.6 select_maximum_fusion
  80.2 14.3 %convolution_bitcast_fusion.24 = f32[32,32]{1,0:T(8,128)} fusion(bf16[1,32,3,130,130]{4,1,3,2,0:T(8,128)(2,1)S(1)} %select_maximum_fusion, bf16[32,128,128]{2,1,0:T(8,128)(2,1)S(1)} %bitcast.360), kind=kOutput, calls=%fused_computation.67 | convolution fusion | flops 33554432 | bytes 2101248 | tf_op jit(solution)/shard_map/dot_general | solution.py:66
  105.9 6.5 copy.71
  112.4 6.9 reshape.605
  119.3 8.9 %copy.72 = bf16[1,32,50700]{1,2,0:T(8,128)(2,1)} copy(bf16[1,32,50700]{2,1,0:T(8,128)(2,1)S(1)} %reshape.605) | data formatting | bytes 6489600 | tf_op jit(solution)/shard_map/reshape | solution.py:78
  128.2 209.4 %gather_fusion = bf16[13824,32]{1,0:T(8,128)(2,1)} fusion(bf16[1,32,50700]{1,2,0:T(8,128)(2,1)} %copy.72, s32[13824]{0:T(1024)S(1)} %fusion.81), kind=kCustom, calls=%fused_computation | custom fusion | bytes 1880064 | tf_op jit(solution)/shard_map/vmap(jit(_take))/gather | solution.py:35
  337.6 3.2 copy.73
  341.0 2.8 fusion.151
  346.5 3.3 copy.74
  349.9 6.1 gather_fusion.1
  356.4 41.9 %psum.23 = f32[32,32]{1,0:T(8,128)S(1)} all-reduce(f32[32,32]{1,0:T(8,128)S(1)} %fusion.34), channel_id=1, replica_groups=mesh['dp'=4,'slab'=8] {'dp','slab'}, use_global_device_ids=true, to_apply=%region_3.4 | all-reduce | flops 1024 | bytes 8192 | tf_op jit(solution)/shard_map/psum | solution.py:89
  400.2 87.7 %all-reduce.7.cloned.1.call-done = (f32[32,864]{1,0:T(8,128)}, f32[864,864]{1,0:T(8,128)}) async-done(((f32[32,864]{1,0:T(8,128)}, f32[864,864]{1,0:T(8,128)}), (f32[32,864]{1,0:T(8,128)}, f32[864,864]{1,0:T(8,128)})) %all-reduce.7.cloned.1.call-update) | async-done | bytes 3096592 | tf_op jit(solution)/shard_map/psum | solution.py:89
  487.8 2.7 select_reduce_fusion
  491.3 1.9 select_add_fusion
  493.2 4.7 copy.75
  497.9 2.3 fusion.6
  500.2 1.6 copy-done.3
  501.8 11.7 %cholesky.204 = f32[128,128]{1,0:T(8,128)S(1)} custom-call(f32[128,128]{1,0:T(8,128)S(1)} %cholesky.534), custom_call_target="Cholesky" | custom-call | tf_op jit(solution)/shard_map/jit(cholesky)/cholesky | solution.py:110
  513.8 9.8 %custom-call.64 = f32[1,128,128]{1,2,0:T(8,128)S(1)} custom-call(f32[1,128,128]{2,1,0:T(8,128)S(1)} %get-tuple-element.40), custom_call_target="InvertDiagBlocksLowerTriangular" | custom-call | tf_op jit(solution)/shard_map/jit(cholesky)/cholesky | solution.py:110
  527.1 13.2 %cholesky.227 = f32[128,128]{1,0:T(8,128)} custom-call(f32[128,128]{1,0:T(8,128)} %cholesky.538), custom_call_target="Cholesky" | custom-call | tf_op jit(solution)/shard_map/jit(cholesky)/cholesky | solution.py:110
  541.8 11.4 %custom-call.65 = f32[1,128,128]{1,2,0:T(8,128)} custom-call(f32[1,128,128]{2,1,0:T(8,128)} %get-tuple-element.37), custom_call_target="InvertDiagBlocksLowerTriangular" | custom-call | tf_op jit(solution)/shard_map/jit(cholesky)/cholesky | solution.py:110
  554.4 1.6 convolution_subtract_fusion.1
  556.1 12.3 %cholesky.432 = f32[128,128]{1,0:T(8,128)} custom-call(f32[128,128]{1,0:T(8,128)S(1)} %cholesky.543), custom_call_target="Cholesky" | custom-call | tf_op jit(solution)/shard_map/jit(cholesky)/cholesky | solution.py:110
  570.0 10.4 %custom-call.66 = f32[1,128,128]{1,2,0:T(8,128)} custom-call(f32[1,128,128]{2,1,0:T(8,128)S(1)} %get-tuple-element.34), custom_call_target="InvertDiagBlocksLowerTriangular" | custom-call | tf_op jit(solution)/shard_map/jit(cholesky)/cholesky | solution.py:110
  581.6 1.7 convolution_subtract_fusion.2
  583.3 11.9 %cholesky.451 = f32[128,128]{1,0:T(8,128)S(1)} custom-call(f32[128,128]{1,0:T(8,128)S(1)} %cholesky.548), custom_call_target="Cholesky" | custom-call | tf_op jit(solution)/shard_map/jit(cholesky)/cholesky | solution.py:110
  596.0 9.8 %custom-call.67 = f32[1,128,128]{1,2,0:T(8,128)S(1)} custom-call(f32[1,128,128]{2,1,0:T(8,128)S(1)} %get-tuple-element.31), custom_call_target="InvertDiagBlocksLowerTriangular" | custom-call | tf_op jit(solution)/shard_map/jit(cholesky)/cholesky | solution.py:110
  606.1 1.7 convolution_subtract_fusion.3
  607.8 11.7 %cholesky.470 = f32[128,128]{1,0:T(8,128)S(1)} custom-call(f32[128,128]{1,0:T(8,128)S(1)} %cholesky.553), custom_call_target="Cholesky" | custom-call | tf_op jit(solution)/shard_map/jit(cholesky)/cholesky | solution.py:110
  620.3 9.8 %custom-call.68 = f32[1,128,128]{1,2,0:T(8,128)S(1)} custom-call(f32[1,128,128]{2,1,0:T(8,128)S(1)} %get-tuple-element.28), custom_call_target="InvertDiagBlocksLowerTriangular" | custom-call | tf_op jit(solution)/shard_map/jit(cholesky)/cholesky | solution.py:110
  631.9 12.1 %cholesky.490 = f32[128,128]{1,0:T(8,128)S(1)} custom-call(f32[128,128]{1,0:T(8,128)S(1)} %cholesky.558), custom_call_target="Cholesky" | custom-call | tf_op jit(solution)/shard_map/jit(cholesky)/cholesky | solution.py:110
  644.6 9.8 %custom-call.69 = f32[1,128,128]{1,2,0:T(8,128)S(1)} custom-call(f32[1,128,128]{2,1,0:T(8,128)S(1)} %get-tuple-element.25), custom_call_target="InvertDiagBlocksLowerTriangular" | custom-call | tf_op jit(solution)/shard_map/jit(cholesky)/cholesky | solution.py:110
  655.8 8.8 %cholesky.511 = f32[96,96]{1,0:T(8,128)S(1)} custom-call(f32[96,96]{1,0:T(8,128)S(1)} %convolution_subtract_fusion.5), custom_call_target="Cholesky" | custom-call | tf_op jit(solution)/shard_map/jit(cholesky)/cholesky | solution.py:110
  672.5 18.0 %while.1 = (s32[]{:T(128)}, f32[864,864]{1,0:T(8,128)}, s32[6,2]{0,1:T(2,128)S(1)}, f32[6,128,128]{2,1,0:T(8,128)S(1)}, s32[]{:T(128)}) while((s32[]{:T(128)}, f32[864,864]{1,0:T(8,128)}, s32[6,2]{0,1:T(2,128)S(1)}, f32[6,128,128]{2,1,0:T(8,128)S(1)}, s32[]{:T(128)}) %tuple.58), condition=%wide.while_cond, body=%wide.while_body.sunk | while | flops 2 | bytes 131181 | solution.py:29
  673.2 2.3 bitcast_dynamic-update-slice_fusion.2
  676.2 2.3 bitcast_dynamic-update-slice_fusion.2
  679.2 2.3 bitcast_dynamic-update-slice_fusion.2
  682.2 2.3 bitcast_dynamic-update-slice_fusion.2
  685.2 2.3 bitcast_dynamic-update-slice_fusion.2
  688.2 2.3 bitcast_dynamic-update-slice_fusion.2
  692.4 69.7 %custom-call.70 = f32[7,128,128]{1,2,0:T(8,128)S(1)} custom-call(f32[7,128,128]{2,1,0:T(8,128)} %pad_maximum_fusion), custom_call_target="InvertDiagBlocksLowerTriangular" | custom-call | tf_op jit(solution)/shard_map/triangular_solve | solution.py:29
  766.2 4.2 cholesky.524
  771.9 2.0 fusion.102
  773.8 3.8 custom-call.71
  (199 shorter events, 76.2 us)
Async XLA Ops:
  7.2 480.6 %all-reduce.7.cloned.1.call-start = ((), (), s32[]{:S(2)}) async-start(), calls=%async_computation | async-start | bytes 6422528 | tf_op jit(solution)/shard_map/psum | solution.py:89
  9.1 49.7 %collective-permute-start = (bf16[1,32,1,128,128]{4,1,3,2,0:T(8,128)(2,1)S(1)}, bf16[1,32,1,128,128]{4,1,3,2,0:T(8,128)(2,1)S(1)}, u32[]{:S(2)}, u32[]{:S(2)}) collective-permute-start(bf16[1,32,1,128,128]{4,1,3,2,0:T(8,128)(2,1)S(1)} %copy.40), channel_id=1, source_target_pairs={{0,1},{1,2},{2,3},{3,4},{4,5},{5,6},{6,7},{8,9},{9,10},{10,11},{11... | collective-permute-start | bytes 3145736 | tf_op jit(solution)/shard_map/ppermute | solution.py:21
  14.1 44.8 %collective-permute-start.1 = (bf16[1,32,1,128,128]{4,1,3,2,0:T(8,128)(2,1)S(1)}, bf16[1,32,1,128,128]{4,1,3,2,0:T(8,128)(2,1)S(1)}, u32[]{:S(2)}, u32[]{:S(2)}) collective-permute-start(bf16[1,32,1,128,128]{4,1,3,2,0:T(8,128)(2,1)S(1)} %copy.40), channel_id=1, source_target_pairs={{1,0},{2,1},{3,2},{4,3},{5,4},{6,5},{7,6},{9,8},{10,9},{11,10},{12... | collective-permute-start | bytes 3145736 | tf_op jit(solution)/shard_map/ppermute | solution.py:22
  21.0 45.5 %copy-start.4 = (bf16[1,32,1,128,128]{4,3,2,1,0:T(8,128)(2,1)S(1)}, bf16[1,32,1,128,128]{4,3,2,1,0:T(8,128)(2,1)}, u32[]{:S(2)}) copy-start(bf16[1,32,1,128,128]{4,3,2,1,0:T(8,128)(2,1)} %param.5) | copy-start | bytes 3145732
  58.9 7.7 copy-start.6
  58.9 7.7 copy-start.8
  340.8 2.9 copy-start.5
  340.8 2.9 copy-start.7
  341.0 3.7 copy-start.9
  343.8 1.8 copy-start.14
  343.8 1.8 copy-start.15
  343.8 1.8 copy-start.16
  343.8 1.8 copy-start.17
  343.8 1.8 copy-start.18
  343.8 1.8 copy-start.19
  343.8 1.8 copy-start.20
  343.8 1.8 copy-start.21
  343.8 1.8 copy-start.22
  343.8 1.8 copy-start.23
  343.9 1.8 copy-start.24
  346.4 3.4 copy-start.25
  398.3 1.9 copy-start.13
  487.8 3.5 copy-start
  500.1 1.6 copy-start.3
  670.6 0.9 copy-start.26
  670.6 1.9 copy-start.12
  670.9 1.7 copy-start.1
  690.5 94.2 %copy-start.2 = (f32[864,864]{1,0:T(8,128)S(1)}, f32[864,864]{1,0:T(8,128)}, u32[]{:S(2)}) copy-start(f32[864,864]{1,0:T(8,128)} %get-tuple-element.120) | copy-start | bytes 8957956
  778.5 11.4 %copy-start.11 = (f32[32,864]{1,0:T(8,128)}, f32[32,864]{1,0:T(8,128)S(1)}, u32[]{:S(2)}) copy-start(f32[32,864]{1,0:T(8,128)S(1)} %broadcast_multiply_fusion) | copy-start | bytes 331780
  778.5 11.4 %copy-start.10 = (f32[32,864]{1,0:T(8,128)S(1)}, f32[32,864]{1,0:T(8,128)}, u32[]{:S(2)}) copy-start(f32[32,864]{1,0:T(8,128)} %get-tuple-element.18) | copy-start | bytes 331780
Sparse Core Ops, SparseCore 0:
  346.6 141.1 all-reduce.6
where the time goes:
time: 800 us; the launch traced here: 799 us
  local copies, waits for them, and re-layouts  276 us (34%)
  other arithmetic  255 us (32%)
  waiting for transfers between devices  125 us (16%)
  matrix products  71.6 us (9%)
  blocking collectives  41.9 us (5%)
  between operations  22 us (3%)
    gather x5, local copies, waits for them, and re-layouts, take_columns(): return jnp.take(matrix, indices, axis=1)  219 us
    another operation x26, other arithmetic, shards(): chol_acts = jnp.linalg.cholesky(damped_activation_factor)  149 us
    psum x1, waiting for transfers between devices, shards(): lax.psum((gram, gradient_gram_matrix, gradient_portion), ('dp', 'slab'))  87.7 us
    another operation x9, other arithmetic, cholesky_apply(): lax.linalg.triangular_solve(factor, halfway, left_side=True, lower=True,...  78.2 us
    dot_general x27, matrix products, shards(): lax.dot_general(grad_rows, shifted, (((0, 2), (0, 2)), ((), ())), preferr...  43.8 us
    psum x1, blocking collectives, shards(): lax.psum((gram, gradient_gram_matrix, gradient_portion), ('dp', 'slab'))  41.9 us
    ppermute x1, waiting for transfers between devices, padded_2(): before = lax.ppermute(last, axis, up)  37.8 us
    another operation x18, local copies, waits for them, and re-layouts  17.9 us
  transfers between devices with their start and end apart: 3, of which 2 were waited for; matrix products, arithmetic and copies ran while one was open for 2% of the time, Pallas kernels for 0%

commit v1 on v0

v1 whole, which is shorter than its diff:
```python
import functools
import math

import jax
import jax.numpy as jnp
from jax import lax
from jax.experimental import pallas as pl
from jax.experimental.pallas import tpu as pltpu
from jax.sharding import PartitionSpec as P

epsilon = 1e-06
damping = 0.1
trust_region_limit = 0.3
learning_rate = 0.01
BLOCK = 128
CHUNK = 1024
NT = (((1,), (1,)), ((), ()))


def local_kernel(width, own, before, after, grads, targets, out, apad, samples, wsum):
    channels, cells = own.shape
    outputs = grads.shape[0]
    per_chunk = targets.shape[0] // 3
    rows = 27 * channels
    total = samples.shape[0]
    third = 9 * channels
    for a, plane in enumerate((before, own, after)):
        apad[a * channels : (a + 1) * channels, width : width + cells] = plane[...]
    apad[:, 0:width] = jnp.zeros((3 * channels, width), apad.dtype)
    apad[:, width + cells :] = jnp.zeros((3 * channels, width), apad.dtype)
    lane = lax.broadcasted_iota(jnp.int32, (outputs, CHUNK), 1) % width
    position = lax.broadcasted_iota(jnp.int32, (3 * per_chunk, CHUNK), 1)
    sums = jnp.zeros((third, 3 * outputs), jnp.float32)
    for k in range(cells // CHUNK):
        base = k * CHUNK
        g = grads[:, base : base + CHUNK]
        wide = g.astype(jnp.float32)
        left = jnp.where(lane == width - 1, 0.0, pltpu.roll(wide, CHUNK - 1, 1)).astype(g.dtype)
        right = jnp.where(lane == 0, 0.0, pltpu.roll(wide, 1, 1)).astype(g.dtype)
        select = jnp.where(position == targets[:, k : k + 1] - base, 1.0, 0.0).astype(g.dtype)
        lhs = jnp.concatenate(
            [apad[:, base + b * width : base + b * width + CHUNK] for b in range(3)] + [g], axis=0
        )
        rhs = jnp.concatenate([left, g, right, select], axis=0)
        both = lax.dot_general(lhs, rhs, NT, preferred_element_type=jnp.float32)
        sums += both[:third, : 3 * outputs]
        where = slice(k * per_chunk, (k + 1) * per_chunk)
        for c in range(3):
            start = 3 * outputs + c * per_chunk
            samples[c * third : (c + 1) * third, where] = both[:third, start : start + per_chunk]
        start = 3 * outputs + per_chunk
        samples[rows : rows + outputs, where] = both[third:, start : start + per_chunk]
    offset = BLOCK - outputs
    for c in range(3):
        wsum[c * third : (c + 1) * third, offset:] = sums[:, c * outputs : (c + 1) * outputs]
    count = total // BLOCK
    r = lax.broadcasted_iota(jnp.int32, (BLOCK, BLOCK), 0)
    l = lax.broadcasted_iota(jnp.int32, (BLOCK, BLOCK), 1)
    vectors = samples[...].astype(jnp.bfloat16)
    slot = 0
    for i in range(count):
        gram = lax.dot_general(
            vectors[i * BLOCK : (i + 1) * BLOCK],
            vectors[i * BLOCK :],
            NT,
            preferred_element_type=jnp.float32,
        )
        for j in range(i, count):
            block = gram[:, (j - i) * BLOCK : (j - i + 1) * BLOCK]
            if j == count - 1:
                weights = wsum[i * BLOCK : (i + 1) * BLOCK, :]
                block = jnp.where((l >= offset) & (r + i * BLOCK < rows), weights, block)
            out[slot] = block
            slot += 1


def split3(value):
    first = value.astype(jnp.bfloat16)
    rest = value - first.astype(jnp.float32)
    second = rest.astype(jnp.bfloat16)
    third = (rest - second.astype(jnp.float32)).astype(jnp.bfloat16)
    return first, second, third


def solve_kernel(
    positions, sample_total, channels, outputs, total, weight_out, update_out,
    a1, a2, a3, pieces, x_ref, r_ref, p_ref, w_ref, inv_ref
):
    rows = 27 * channels
    size = a1.shape[0]
    count = size // BLOCK
    offset = BLOCK - outputs
    r = lax.broadcasted_iota(jnp.int32, (BLOCK, BLOCK), 0)
    l = lax.broadcasted_iota(jnp.int32, (BLOCK, BLOCK), 1)
    slots = {}
    for i in range(count):
        for j in range(i, count):
            slots[i, j] = len(slots)
    diagonals = [
        jnp.sum(jnp.where(r == l, total[slots[i, i]], 0.0), axis=1, keepdims=True)
        for i in range(count)
    ]
    column = lax.broadcasted_iota(jnp.int32, (BLOCK, 1), 0)
    trace_a = jnp.zeros((1, 1), jnp.float32)
    trace_g = jnp.zeros((1, 1), jnp.float32)
    for i in range(count):
        inside = column + i * BLOCK < rows
        trace_a += jnp.sum(jnp.where(inside, diagonals[i], 0.0), axis=0, keepdims=True)
        trace_g += jnp.sum(jnp.where(inside, 0.0, diagonals[i]), axis=0, keepdims=True)
    ratio = jnp.sqrt(
        (trace_a / sample_total / rows + epsilon) / (trace_g / sample_total / outputs + epsilon)
    )
    shift_a = ratio * math.sqrt(damping)
    shift_g = math.sqrt(damping) / ratio
    for i in range(count):
        inside = column + i * BLOCK < rows
        inv_ref[i * BLOCK : (i + 1) * BLOCK, :] = 1.0 / jnp.where(
            inside, diagonals[i] / sample_total + shift_a, 1.0
        )
        for j in range(i, count):
            block = total[slots[i, j]] / sample_total
            if j == count - 1:
                w_ref[i * BLOCK : (i + 1) * BLOCK, :] = (
                    total[slots[i, j]][:, offset:] / math.sqrt(positions)
                )
                block = jnp.where((r + i * BLOCK < rows) & (l + j * BLOCK < rows), block, 0.0)
            if i == j:
                shift = jnp.where(r + i * BLOCK < rows, shift_a, 1.0)
                block = jnp.where(r == l, block + shift, block)
            here = (slice(i * BLOCK, (i + 1) * BLOCK), slice(j * BLOCK, (j + 1) * BLOCK))
            for ref, part in zip((a1, a2, a3), split3(block)):
                ref[here] = part
            if i != j:
                for ref, part in zip((a1, a2, a3), split3(block.T)):
                    ref[here[1], here[0]] = part
    w_ref[rows:, :] = jnp.zeros((size - rows, outputs), jnp.float32)

    gr = lax.broadcasted_iota(jnp.int32, (outputs, outputs), 0)
    gc = lax.broadcasted_iota(jnp.int32, (outputs, outputs), 1)
    factor = total[slots[count - 1, count - 1]][offset:, offset:] / sample_total
    factor = jnp.where(gr == gc, factor + shift_g, factor)

    def eliminate(k, m):
        row = jnp.sum(jnp.where(gr == k, m, 0.0), axis=0, keepdims=True)
        col = jnp.sum(jnp.where(gc == k, m, 0.0), axis=1, keepdims=True)
        pivot = jnp.sum(jnp.where(gr[:, :1] == k, col, 0.0), axis=0, keepdims=True)
        inverse = 1.0 / pivot
        scaled = row * inverse
        rest = m - col * scaled
        rest = jnp.where(gr == k, scaled, rest)
        rest = jnp.where(gc == k, -col * inverse, rest)
        return jnp.where((gr == k) & (gc == k), inverse, rest)

    inverse_g = lax.fori_loop(0, outputs, eliminate, factor)
    weights = w_ref[...]
    rhs = jnp.dot(
        weights, inverse_g, precision=lax.Precision.HIGHEST, preferred_element_type=jnp.float32
    )
    top = jnp.max(jnp.abs(rhs), axis=0, keepdims=True)
    top = jnp.where(top > 0.0, top, 1.0)
    residual = rhs / top
    x_ref[...] = jnp.zeros_like(x_ref)
    r_ref[...] = residual
    z = residual * inv_ref[...]
    p_ref[...] = z
    rz0 = jnp.sum(residual * z, axis=0, keepdims=True)
    goal = rz0 * 1e-16

    def unfinished(state):
        step, rz = state
        return (jnp.max(jnp.where(rz > goal, 1.0, 0.0)) > 0.0) & (step < 8 * size)

    def iterate(state):
        step, rz = state
        p = p_ref[...]
        for n, part in enumerate(split3(p)):
            pieces[:, n * outputs : (n + 1) * outputs] = part
        product = jnp.dot(a1[...], pieces[...], preferred_element_type=jnp.float32)
        second = jnp.dot(a2[...], pieces[:, : 2 * outputs], preferred_element_type=jnp.float32)
        third = jnp.dot(a3[...], pieces[:, :outputs], preferred_element_type=jnp.float32)
        q = (
            product[:, 2 * outputs :] + second[:, outputs:] + third
        ) + (product[:, outputs : 2 * outputs] + second[:, :outputs]) + product[:, :outputs]
        pq = jnp.sum(p * q, axis=0, keepdims=True)
        alpha = jnp.where(pq > 0.0, rz / jnp.where(pq > 0.0, pq, 1.0), 0.0)
        x_ref[...] += alpha * p
        left = r_ref[...] - alpha * q
        r_ref[...] = left
        preconditioned = left * inv_ref[...]
        after = jnp.sum(left * preconditioned, axis=0, keepdims=True)
        beta = jnp.where(rz > 0.0, after / jnp.where(rz > 0.0, rz, 1.0), 0.0)
        p_ref[...] = preconditioned + beta * p
        return step + 1, after

    lax.while_loop(unfinished, iterate, (jnp.int32(0), rz0))
    precond = x_ref[...] * top
    quadratic = jnp.sum(
        jnp.sum(precond * weights, axis=0, keepdims=True), axis=1, keepdims=True
    )
    clip = jnp.minimum(1.0, jnp.sqrt(trust_region_limit / (learning_rate**2 * quadratic)))
    flat_w = weights.T
    flat_u = (precond * clip).T
    for c in range(3):
        for b in range(3):
            for a in range(3):
                source = (c * 9 + b * 3 + a) * channels
                dest = (a * 9 + b * 3 + c) * channels
                weight_out[:, dest : dest + channels] = flat_w[:, source : source + channels]
                update_out[:, dest : dest + channels] = flat_u[:, source : source + channels]


def halo(plane):
    size = lax.axis_size("slab")
    pairs = [(i, i ^ 1) for i in range(size) if i ^ 1 < size]
    relays = [(i, i + 2) for i in range(0, size - 2, 2)] + [(i, i - 2) for i in range(3, size, 2)]
    swapped, relayed = [], []
    for part in jnp.split(plane, 4, axis=0):
        got = lax.ppermute(part, "slab", pairs)
        swapped.append(got)
        relayed.append(lax.ppermute(got, "slab", relays))
    swapped = jnp.concatenate(swapped, axis=0)
    relayed = jnp.concatenate(relayed, axis=0)
    even = lax.axis_index("slab") % 2 == 0
    return jnp.where(even, relayed, swapped), jnp.where(even, swapped, relayed)


def shards(acts, grads, picks):
    volumes, channels, planes, height, width = acts.shape
    outputs = grads.shape[1]
    cells = height * width
    own = acts.reshape(channels, cells)
    rows = grads.reshape(outputs, cells)
    before, after = halo(own)
    samples = picks.shape[1]
    chunks = cells // CHUNK
    position = jnp.arange(samples, dtype=jnp.int32) * 32 + picks.reshape(samples)
    column = position % width
    targets = jnp.stack(
        [
            jnp.where((column + d >= 0) & (column + d < width), position + d, -1)
            for d in (-1, 0, 1)
        ]
    )
    targets = targets.reshape(3, chunks, samples // chunks).transpose(0, 2, 1)
    targets = targets.reshape(3 * (samples // chunks), chunks)
    size = 27 * channels + outputs
    count = size // BLOCK
    blocks = count * (count + 1) // 2
    partial = pl.pallas_call(
        functools.partial(local_kernel, width),
        out_shape=jax.ShapeDtypeStruct((blocks, BLOCK, BLOCK), jnp.float32),
        in_specs=[pl.BlockSpec(memory_space=pltpu.VMEM)] * 5,
        out_specs=pl.BlockSpec(memory_space=pltpu.VMEM),
        scratch_shapes=[
            pltpu.VMEM((3 * channels, cells + 2 * width), jnp.bfloat16),
            pltpu.VMEM((size, samples), jnp.float32),
            pltpu.VMEM((size, BLOCK), jnp.float32),
        ],
        compiler_params=pltpu.CompilerParams(vmem_limit_bytes=48 * 1024 * 1024),
        name="local_sums",
    )(own, before, after, rows, targets)
    total = lax.psum(partial, ("dp", "slab"))
    everyone = lax.axis_size("dp") * lax.axis_size("slab") * volumes
    return pl.pallas_call(
        functools.partial(
            solve_kernel, everyone * planes * cells, everyone * samples, channels, outputs
        ),
        out_shape=[jax.ShapeDtypeStruct((outputs, 27 * channels), jnp.float32)] * 2,
        in_specs=[pl.BlockSpec(memory_space=pltpu.VMEM)],
        out_specs=[pl.BlockSpec(memory_space=pltpu.VMEM)] * 2,
        scratch_shapes=[pltpu.VMEM((size, size), jnp.bfloat16)] * 3
        + [pltpu.VMEM((size, 3 * outputs), jnp.bfloat16)]
        + [pltpu.VMEM((size, outputs), jnp.float32)] * 4
        + [pltpu.VMEM((size, 1), jnp.float32)],
        compiler_params=pltpu.CompilerParams(vmem_limit_bytes=48 * 1024 * 1024),
        name="solve",
    )(total)


def solution(mesh):
    return jax.shard_map(
        shards,
        mesh=mesh,
        in_specs=(
            P("dp", None, "slab", None, None),
            P("dp", None, "slab", None, None),
            P("dp", "slab"),
        ),
        out_specs=(P(), P()),
        check_vma=False,
    )
```

time: 800 us -> 260 us (0.33)
  local copies, waits for them, and re-layouts: 276 us -> 7.66 us
  other arithmetic: 255 us -> 0.2 us
  matrix products: 71.6 us -> 0 us
  Pallas kernels: 0 us -> 71.6 us
  blocking collectives: 41.9 us -> 0 us
  waiting for transfers between devices: 125 us -> 145 us
  starting transfers between devices: 6.27 us -> 20.9 us
    another operation x38 -> x1, other arithmetic: 233 us -> 0.01 us  [shards(): jnp.stack([jnp.where((column + d >= 0) & (column + d < width), position +...]
    gather x5 -> x0, local copies, waits for them, and re-layouts: 219 us -> none  [take_columns(): return jnp.take(matrix, indices, axis=1)]
    pallas_call x0 -> x2, Pallas kernels: none -> 71.6 us  [the longest x1 65.9 us: shards(): pl.pallas_call(functools.partial(solve_kernel, everyone * planes * cells,...]
    psum x1, waiting for transfers between devices: 87.7 us -> 135 us  [shards(): total = lax.psum(partial, ('dp', 'slab'))]
    dot_general x29 -> x0, matrix products: 46.9 us -> none  [the longest x27 43.8 us: shards(): lax.dot_general(grad_rows, shifted, (((0, 2), (0, 2)), ((), ())), preferr...]
    psum x1 -> x0, blocking collectives: 41.9 us -> none  [shards(): lax.psum((gram, gradient_gram_matrix, gradient_portion), ('dp', 'slab'))]
    ppermute x2 -> x8, waiting for transfers between devices: 37.8 us -> 10.1 us  [the longest x4 5.29 us: halo(): got = lax.ppermute(part, 'slab', pairs)]
    another operation x40 -> x0, matrix products: 24.7 us -> none  [the longest x12 13.7 us: shards(): chol_acts = jnp.linalg.cholesky(damped_activation_factor)]
  transfers between devices with their start and end apart: 3 -> 9, of which waited for: 2 -> 6; matrix products, arithmetic and copies ran while one was open for 2% -> 2% of each run, Pallas kernels for 0% -> 0%
where the time goes in v1:
time: 260 us
  waiting for transfers between devices  145 us (56%)
  Pallas kernels  71.6 us (28%)
  starting transfers between devices  20.9 us (8%)
  between operations  14.2 us (5%)
  local copies, waits for them, and re-layouts  7.66 us (3%)
    psum x1, waiting for transfers between devices, shards(): total = lax.psum(partial, ('dp', 'slab'))  135 us
    pallas_call x1, Pallas kernels, shards(): pl.pallas_call(functools.partial(solve_kernel, everyone * planes * cells,...  65.9 us
    ppermute x4, starting transfers between devices, halo(): relayed.append(lax.ppermute(got, 'slab', relays))  15.8 us
    unnamed x21, local copies, waits for them, and re-layouts  7.17 us
    pallas_call x1, Pallas kernels, shards(): pl.pallas_call(functools.partial(local_kernel, width), out_shape=jax.Shap...  5.69 us
    ppermute x4, waiting for transfers between devices, halo(): got = lax.ppermute(part, 'slab', pairs)  5.29 us
  transfers between devices with their start and end apart: 9, of which 6 were waited for; matrix products, arithmetic and copies ran while one was open for 2% of the time, Pallas kernels for 0%

profile of v1, /device:TPU:0, one launch (start us, length us, event | category | flops | bytes accessed | tf_op | source)
XLA Modules:
  0.0 259.6 jit_solution(11402479250787247120)
XLA Ops:
  7.2 0.0 copy-start.3
  7.2 0.0 copy-start.2
  7.2 0.0 all-reduce.2.cloned.1.call-start
  7.2 1.4 slice_bitcast_fusion
  8.6 0.9 copy.25
  9.5 3.0 %collective-permute-start = (bf16[8,16384]{1,0:T(8,128)(2,1)}, bf16[8,16384]{1,0:T(8,128)(2,1)S(1)}, u32[]{:S(2)}, u32[]{:S(2)}) collective-permute-start(bf16[8,16384]{1,0:T(8,128)(2,1)} %bitcast.36), channel_id=1, source_target_pairs={{0,1},{1,0},{2,3},{3,2},{4,5},{5,4},{6,7},{7,6},{8,9},{9,8},{10,11... | collective-permute-start | bytes 786440 | tf_op jit(solution)/shard_map/ppermute | solution.py:218
  12.5 0.0 copy-start.1
  12.5 0.9 copy.24
  13.3 0.0 collective-permute-start.2
  13.3 0.9 copy.23
  14.2 2.0 collective-permute-start.4
  16.2 0.2 copy.22
  16.4 0.1 collective-permute-start.6
  16.5 0.0 copy-done.3
  16.6 0.1 stack.12
  16.6 0.1 copy.5
  16.7 0.1 stack.13
  16.8 0.1 copy.6
  16.9 0.1 stack.14
  16.9 0.1 copy.7
  17.0 0.0 copy-done.2
  17.0 0.7 copy.20
  17.7 0.0 copy-done.1
  17.7 0.7 copy.21
  18.4 1.4 collective-permute-done
  19.8 4.0 %collective-permute-start.1 = (bf16[8,16384]{1,0:T(8,128)(2,1)S(1)}, bf16[8,16384]{1,0:T(8,128)(2,1)S(1)}, u32[]{:S(2)}, u32[]{:S(2)}) collective-permute-start(bf16[8,16384]{1,0:T(8,128)(2,1)S(1)} %collective-permute-done), channel_id=1, source_target_pairs={{0,2},{2,4},{4,6},{3,1},{5,3},{7,5},{8,10},{10,12},{12,14},{11,9},... | collective-permute-start | bytes 786440 | tf_op jit(solution)/shard_map/ppermute | solution.py:220
  23.9 1.6 collective-permute-done.2
  25.4 4.0 %collective-permute-start.3 = (bf16[8,16384]{1,0:T(8,128)(2,1)S(1)}, bf16[8,16384]{1,0:T(8,128)(2,1)S(1)}, u32[]{:S(2)}, u32[]{:S(2)}) collective-permute-start(bf16[8,16384]{1,0:T(8,128)(2,1)S(1)} %collective-permute-done.2), channel_id=1, source_target_pairs={{0,2},{2,4},{4,6},{3,1},{5,3},{7,5},{8,10},{10,12},{12,14},{11,9},... | collective-permute-start | bytes 786440 | tf_op jit(solution)/shard_map/ppermute | solution.py:220
  29.5 1.6 collective-permute-done.4
  31.1 4.0 %collective-permute-start.5 = (bf16[8,16384]{1,0:T(8,128)(2,1)S(1)}, bf16[8,16384]{1,0:T(8,128)(2,1)S(1)}, u32[]{:S(2)}, u32[]{:S(2)}) collective-permute-start(bf16[8,16384]{1,0:T(8,128)(2,1)S(1)} %collective-permute-done.4), channel_id=1, source_target_pairs={{0,2},{2,4},{4,6},{3,1},{5,3},{7,5},{8,10},{10,12},{12,14},{11,9},... | collective-permute-start | bytes 786440 | tf_op jit(solution)/shard_map/ppermute | solution.py:220
  35.1 0.7 collective-permute-done.6
  35.8 3.7 %collective-permute-start.7 = (bf16[8,16384]{1,0:T(8,128)(2,1)S(1)}, bf16[8,16384]{1,0:T(8,128)(2,1)S(1)}, u32[]{:S(2)}, u32[]{:S(2)}) collective-permute-start(bf16[8,16384]{1,0:T(8,128)(2,1)S(1)} %collective-permute-done.6), channel_id=1, source_target_pairs={{0,2},{2,4},{4,6},{3,1},{5,3},{7,5},{8,10},{10,12},{12,14},{11,9},... | collective-permute-start | bytes 786440 | tf_op jit(solution)/shard_map/ppermute | solution.py:220
  39.6 0.0 collective-permute-done.1
  39.7 0.0 collective-permute-done.3
  39.7 0.0 collective-permute-done.5
  39.8 4.8 %collective-permute-done.7 = bf16[8,16384]{1,0:T(8,128)(2,1)S(1)} collective-permute-done((bf16[8,16384]{1,0:T(8,128)(2,1)S(1)}, bf16[8,16384]{1,0:T(8,128)(2,1)S(1)}, u32[]{:S(2)}, u32[]{:S(2)}) %collective-permute-start.7) | collective-permute-done | bytes 262176 | tf_op jit(solution)/shard_map/ppermute | solution.py:220
  44.6 0.1 broadcast_select_fusion
  44.7 5.7 %local_sums.1 = f32[28,128,128]{2,1,0:T(8,128)} custom-call(bf16[32,16384]{1,0:T(8,128)(2,1)S(1)} %bitcast.38, bf16[32,16384]{1,0:T(8,128)(2,1)S(1)} %get-tuple-element.6.before, bf16[32,16384]{1,0:T(8,128)(2,1)S(1)} %get-tuple-element.5.after, bf16[32,16384]{1,0:T(8,128)(2,1)S(1)} %bitcast.37, s32[96,16]{1,0:T(8,128)S(1)} %bitcast.39), custom_call_target="tpu_custom_call" | custom-call | tf_op jit(solution)/shard_map/local_sums/pallas_call | solution.py:249
  50.4 0.0 all-reduce.2.cloned.1.call-update
  50.4 134.9 %all-reduce.2.cloned.1.call-done.total = f32[28,128,128]{2,1,0:T(8,128)} async-done(((f32[28,128,128]{2,1,0:T(8,128)}), f32[28,128,128]{2,1,0:T(8,128)}) %all-reduce.2.cloned.1.call-update) | async-done | bytes 1835024 | tf_op jit(solution)/shard_map/psum | solution.py:262
  185.3 0.0 copy-start
  185.3 1.5 copy-done
  186.8 65.9 %solve.1 = (f32[32,864]{1,0:T(8,128)}, f32[32,864]{1,0:T(8,128)}) custom-call(f32[28,128,128]{2,1,0:T(8,128)S(1)} %copy-done), custom_call_target="tpu_custom_call" | custom-call | tf_op jit(solution)/shard_map/solve/pallas_call | solution.py:264
  (10 shorter events, 0.2 us)
Async XLA Ops:
  7.2 9.3 %copy-start.3 = (s32[1,512]{1,0:T(1,128)S(1)}, s32[1,512]{1,0:T(1,128)}, u32[]{:S(2)}) copy-start(s32[1,512]{1,0:T(1,128)} %param.5) | copy-start | bytes 6148
  7.2 9.8 %copy-start.2 = (bf16[1,32,1,128,128]{4,3,2,1,0:T(8,128)(2,1)S(1)}, bf16[1,32,1,128,128]{4,3,2,1,0:T(8,128)(2,1)}, u32[]{:S(2)}) copy-start(bf16[1,32,1,128,128]{4,3,2,1,0:T(8,128)(2,1)} %param.4) | copy-start | bytes 3145732
  7.2 178.2 %all-reduce.2.cloned.1.call-start = ((), (), s32[]{:S(2)}) async-start(), calls=%async_computation | async-start | bytes 3670016 | tf_op jit(solution)/shard_map/psum | solution.py:262
  9.5 10.3 %collective-permute-start = (bf16[8,16384]{1,0:T(8,128)(2,1)}, bf16[8,16384]{1,0:T(8,128)(2,1)S(1)}, u32[]{:S(2)}, u32[]{:S(2)}) collective-permute-start(bf16[8,16384]{1,0:T(8,128)(2,1)} %bitcast.36), channel_id=1, source_target_pairs={{0,1},{1,0},{2,3},{3,2},{4,5},{5,4},{6,7},{7,6},{8,9},{9,8},{10,11... | collective-permute-start | bytes 786440 | tf_op jit(solution)/shard_map/ppermute | solution.py:218
  12.5 5.3 %copy-start.1 = (bf16[1,32,1,128,128]{4,3,2,1,0:T(8,128)(2,1)S(1)}, bf16[1,32,1,128,128]{4,3,2,1,0:T(8,128)(2,1)}, u32[]{:S(2)}) copy-start(bf16[1,32,1,128,128]{4,3,2,1,0:T(8,128)(2,1)} %param.3) | copy-start | bytes 3145732
  13.3 12.1 %collective-permute-start.2 = (bf16[8,16384]{1,0:T(8,128)(2,1)}, bf16[8,16384]{1,0:T(8,128)(2,1)S(1)}, u32[]{:S(2)}, u32[]{:S(2)}) collective-permute-start(bf16[8,16384]{1,0:T(8,128)(2,1)} %bitcast.35), channel_id=1, source_target_pairs={{0,1},{1,0},{2,3},{3,2},{4,5},{5,4},{6,7},{7,6},{8,9},{9,8},{10,11... | collective-permute-start | bytes 786440 | tf_op jit(solution)/shard_map/ppermute | solution.py:218
  14.2 16.8 %collective-permute-start.4 = (bf16[8,16384]{1,0:T(8,128)(2,1)}, bf16[8,16384]{1,0:T(8,128)(2,1)S(1)}, u32[]{:S(2)}, u32[]{:S(2)}) collective-permute-start(bf16[8,16384]{1,0:T(8,128)(2,1)} %bitcast.34), channel_id=1, source_target_pairs={{0,1},{1,0},{2,3},{3,2},{4,5},{5,4},{6,7},{7,6},{8,9},{9,8},{10,11... | collective-permute-start | bytes 786440 | tf_op jit(solution)/shard_map/ppermute | solution.py:218
  16.4 19.4 %collective-permute-start.6 = (bf16[8,16384]{1,0:T(8,128)(2,1)S(1)}, bf16[8,16384]{1,0:T(8,128)(2,1)S(1)}, u32[]{:S(2)}, u32[]{:S(2)}) collective-permute-start(bf16[8,16384]{1,0:T(8,128)(2,1)S(1)} %bitcast.42), channel_id=1, source_target_pairs={{0,1},{1,0},{2,3},{3,2},{4,5},{5,4},{6,7},{7,6},{8,9},{9,8},{10,11... | collective-permute-start | bytes 786440 | tf_op jit(solution)/shard_map/ppermute | solution.py:218
  19.8 19.8 %collective-permute-start.1 = (bf16[8,16384]{1,0:T(8,128)(2,1)S(1)}, bf16[8,16384]{1,0:T(8,128)(2,1)S(1)}, u32[]{:S(2)}, u32[]{:S(2)}) collective-permute-start(bf16[8,16384]{1,0:T(8,128)(2,1)S(1)} %collective-permute-done), channel_id=1, source_target_pairs={{0,2},{2,4},{4,6},{3,1},{5,3},{7,5},{8,10},{10,12},{12,14},{11,9},... | collective-permute-start | bytes 786440 | tf_op jit(solution)/shard_map/ppermute | solution.py:220
  25.4 14.3 %collective-permute-start.3 = (bf16[8,16384]{1,0:T(8,128)(2,1)S(1)}, bf16[8,16384]{1,0:T(8,128)(2,1)S(1)}, u32[]{:S(2)}, u32[]{:S(2)}) collective-permute-start(bf16[8,16384]{1,0:T(8,128)(2,1)S(1)} %collective-permute-done.2), channel_id=1, source_target_pairs={{0,2},{2,4},{4,6},{3,1},{5,3},{7,5},{8,10},{10,12},{12,14},{11,9},... | collective-permute-start | bytes 786440 | tf_op jit(solution)/shard_map/ppermute | solution.py:220
  31.1 8.7 %collective-permute-start.5 = (bf16[8,16384]{1,0:T(8,128)(2,1)S(1)}, bf16[8,16384]{1,0:T(8,128)(2,1)S(1)}, u32[]{:S(2)}, u32[]{:S(2)}) collective-permute-start(bf16[8,16384]{1,0:T(8,128)(2,1)S(1)} %collective-permute-done.4), channel_id=1, source_target_pairs={{0,2},{2,4},{4,6},{3,1},{5,3},{7,5},{8,10},{10,12},{12,14},{11,9},... | collective-permute-start | bytes 786440 | tf_op jit(solution)/shard_map/ppermute | solution.py:220
  35.8 8.7 %collective-permute-start.7 = (bf16[8,16384]{1,0:T(8,128)(2,1)S(1)}, bf16[8,16384]{1,0:T(8,128)(2,1)S(1)}, u32[]{:S(2)}, u32[]{:S(2)}) collective-permute-start(bf16[8,16384]{1,0:T(8,128)(2,1)S(1)} %collective-permute-done.6), channel_id=1, source_target_pairs={{0,2},{2,4},{4,6},{3,1},{5,3},{7,5},{8,10},{10,12},{12,14},{11,9},... | collective-permute-start | bytes 786440 | tf_op jit(solution)/shard_map/ppermute | solution.py:220
  185.3 1.5 copy-start
Sparse Core Ops, SparseCore 0:
  50.6 134.7 all-reduce.1

commit v2 on v1

--- a/solution.py
+++ b/solution.py
@@ -209,6 +209,133 @@
                 update_out[:, dest : dest + channels] = flat_u[:, source : source + channels]
 
 
+MESH = pl.DeviceIdType.MESH
+
+
+def bit_orders(dp, slab):
+    core = [("dp", 1)] if dp > 1 else []
+    along_y = [("dp", 1 << n) for n in range(1, dp.bit_length() - 1)]
+    along_x = [("slab", 1)] if slab > 1 else []
+    along_z = [("slab", 1 << n) for n in range(1, slab.bit_length() - 1)]
+    groups = [along_x, along_y, along_z]
+    return [core + groups[n] + groups[(n + 1) % 3] + groups[(n + 2) % 3] for n in range(3)]
+
+
+def portion_plan(rows, orders):
+    unit = rows // 14
+    sizes = [5 * unit, 5 * unit, rows - 10 * unit]
+    plan, start = [], 0
+    for size, order in zip(sizes, orders):
+        stages, length = [], size
+        for bit in order:
+            halves = length % 16 == 0
+            length = length // 2 if halves else length
+            stages.append((bit, length, halves))
+        plan.append((start, size, stages))
+        start += size
+    return plan
+
+
+def sum_kernel(plan, value, out, work, *scratch):
+    stages = len(plan[0][2])
+    recv = [scratch[n * stages : (n + 1) * stages] for n in range(len(plan))]
+    send_sem, recv_sem = scratch[len(plan) * stages :]
+    me = {"dp": lax.axis_index("dp"), "slab": lax.axis_index("slab")}
+
+    def bit_of(bit):
+        return (me[bit[0]] // bit[1]) % 2
+
+    def partner(bit):
+        there = dict(me)
+        there[bit[0]] = me[bit[0]] + bit[1] * (1 - 2 * bit_of(bit))
+        return (there["dp"], there["slab"])
+
+    barrier = pltpu.get_barrier_semaphore()
+    for bit, _, _ in plan[0][2]:
+        pl.semaphore_signal(barrier, inc=1, device_id=partner(bit), device_id_type=MESH)
+    pl.semaphore_wait(barrier, stages)
+
+    first = [[start] for start, _, _ in plan]
+
+    def window(start, length):
+        return pl.ds(pl.multiple_of(start, 8), length)
+
+    def begin(n, s):
+        bit, length, halves = plan[n][2][s]
+        before = first[n][s]
+        mine = before + bit_of(bit) * length if halves else before
+        other = before + (1 - bit_of(bit)) * length if halves else before
+        first[n].append(mine)
+        source = value if s == 0 else work
+        copy = pltpu.make_async_remote_copy(
+            src_ref=source.at[window(other, length)],
+            dst_ref=recv[n][s],
+            send_sem=send_sem.at[0, n, s],
+            recv_sem=recv_sem.at[0, n, s],
+            device_id=partner(bit),
+            device_id_type=MESH,
+        )
+        copy.start()
+        return copy
+
+    flying = [begin(n, 0) for n in range(len(plan))]
+    for s in range(stages):
+        for n in range(len(plan)):
+            _, length, _ = plan[n][2][s]
+            flying[n].wait()
+            here = window(first[n][s + 1], length)
+            source = value if s == 0 else work
+            target = work if s + 1 < stages else out
+            target[here, :] = source[here, :] + recv[n][s][...]
+            if s + 1 < stages:
+                flying[n] = begin(n, s + 1)
+
+    def spread(n, s):
+        bit, length, _ = plan[n][2][s]
+        here = window(first[n][s + 1], length)
+        copy = pltpu.make_async_remote_copy(
+            src_ref=out.at[here],
+            dst_ref=out.at[here],
+            send_sem=send_sem.at[1, n, s],
+            recv_sem=recv_sem.at[1, n, s],
+            device_id=partner(bit),
+            device_id_type=MESH,
+        )
+        copy.start()
+        return copy
+
+    back = [[s for s in range(stages - 1, -1, -1) if stage[2][s][2]] for stage in plan]
+    flying = [spread(n, back[n][0]) for n in range(len(plan))]
+    for step in range(max(len(b) for b in back)):
+        for n in range(len(plan)):
+            if step < len(back[n]):
+                flying[n].wait()
+                if step + 1 < len(back[n]):
+                    flying[n] = spread(n, back[n][step + 1])
+
+
+def sum_everywhere(value):
+    rows, lanes = value.shape
+    plan = portion_plan(rows, bit_orders(lax.axis_size("dp"), lax.axis_size("slab")))
+    stages = len(plan[0][2])
+    buffers = [
+        pltpu.VMEM((length, lanes), value.dtype) for _, _, steps in plan for _, length, _ in steps
+    ]
+    return pl.pallas_call(
+        functools.partial(sum_kernel, plan),
+        out_shape=jax.ShapeDtypeStruct(value.shape, value.dtype),
+        in_specs=[pl.BlockSpec(memory_space=pltpu.VMEM)],
+        out_specs=pl.BlockSpec(memory_space=pltpu.VMEM),
+        scratch_shapes=[pltpu.VMEM(value.shape, value.dtype)]
+        + buffers
+        + [pltpu.SemaphoreType.DMA((2, len(plan), stages))] * 2,
+        compiler_params=pltpu.CompilerParams(
+            collective_id=0, has_side_effects=True, vmem_limit_bytes=24 * 1024 * 1024
+        ),
+        name="sum_everywhere",
+    )(value)
+
+
 def halo(plane):
     size = lax.axis_size("slab")
     pairs = [(i, i ^ 1) for i in range(size) if i ^ 1 < size]
@@ -259,7 +386,7 @@
         compiler_params=pltpu.CompilerParams(vmem_limit_bytes=48 * 1024 * 1024),
         name="local_sums",
     )(own, before, after, rows, targets)
-    total = lax.psum(partial, ("dp", "slab"))
+    total = sum_everywhere(partial.reshape(-1, BLOCK)).reshape(partial.shape)
     everyone = lax.axis_size("dp") * lax.axis_size("slab") * volumes
     return pl.pallas_call(
         functools.partial(

time: 260 us -> 148 us (0.57); the launches traced: 260 us -> 150 us
  waiting for transfers between devices: 145 us -> 10.1 us
  Pallas kernels: 71.6 us -> 112 us
  between operations: 14.2 us -> 0.86 us
    psum x1 -> x0, waiting for transfers between devices: 135 us -> none  [shards(): total = lax.psum(partial, ('dp', 'slab'))]
    pallas_call x0 -> x1, Pallas kernels: none -> 41.9 us  [sum_everywhere(): pl.pallas_call(functools.partial(sum_kernel, plan), out_shape=jax.ShapeDt...]
    unnamed x21 -> x19, local copies, waits for them, and re-layouts: 7.17 us -> 5.66 us
  transfers between devices with their start and end apart: 9 -> 8, of which waited for: 6 -> 5; matrix products, arithmetic and copies ran while one was open for 2% -> 3% of each run, Pallas kernels for 0% -> 0%
where the time goes in v2:
time: 148 us; the launch traced here: 150 us
  Pallas kernels  112 us (76%)
  starting transfers between devices  20.9 us (14%)
  waiting for transfers between devices  10.1 us (7%)
  local copies, waits for them, and re-layouts  6.15 us (4%)
    pallas_call x1, Pallas kernels, shards(): pl.pallas_call(functools.partial(solve_kernel, everyone * planes * cells,...  65.9 us
    pallas_call x1, Pallas kernels, sum_everywhere(): pl.pallas_call(functools.partial(sum_kernel, plan), out_shape=jax.ShapeDt...  41.9 us
    ppermute x4, starting transfers between devices, halo(): relayed.append(lax.ppermute(got, 'slab', relays))  15.8 us
    unnamed x19, local copies, waits for them, and re-layouts  5.66 us
    ppermute x4, waiting for transfers between devices, halo(): got = lax.ppermute(part, 'slab', pairs)  5.3 us
    ppermute x4, starting transfers between devices, halo(): got = lax.ppermute(part, 'slab', pairs)  5.06 us
    ppermute x4, waiting for transfers between devices, halo(): relayed.append(lax.ppermute(got, 'slab', relays))  4.8 us
    pallas_call x1, Pallas kernels, shards(): pl.pallas_call(functools.partial(local_kernel, width), out_shape=jax.Shap...  4.46 us
  transfers between devices with their start and end apart: 8, of which 5 were waited for; matrix products, arithmetic and copies ran while one was open for 3% of the time, Pallas kernels for 0%

profile of v2, /device:TPU:0, one launch (start us, length us, event | category | flops | bytes accessed | tf_op | source)
XLA Modules:
  0.0 150.5 jit_solution(16092427496412423223)
XLA Ops:
  0.6 0.0 copy-start.2
  0.6 0.0 copy-start.1
  0.6 1.4 slice_bitcast_fusion
  2.0 0.9 copy.25
  2.9 3.0 %collective-permute-start = (bf16[8,16384]{1,0:T(8,128)(2,1)}, bf16[8,16384]{1,0:T(8,128)(2,1)S(1)}, u32[]{:S(2)}, u32[]{:S(2)}) collective-permute-start(bf16[8,16384]{1,0:T(8,128)(2,1)} %bitcast.38), channel_id=1, source_target_pairs={{0,1},{1,0},{2,3},{3,2},{4,5},{5,4},{6,7},{7,6},{8,9},{9,8},{10,11... | collective-permute-start | bytes 786440 | tf_op jit(solution)/shard_map/ppermute | solution.py:345
  5.9 0.0 copy-start
  5.9 0.9 copy.24
  6.8 0.0 collective-permute-start.2
  6.8 0.9 copy.23
  7.6 2.0 %collective-permute-start.4 = (bf16[8,16384]{1,0:T(8,128)(2,1)}, bf16[8,16384]{1,0:T(8,128)(2,1)S(1)}, u32[]{:S(2)}, u32[]{:S(2)}) collective-permute-start(bf16[8,16384]{1,0:T(8,128)(2,1)} %bitcast.36), channel_id=1, source_target_pairs={{0,1},{1,0},{2,3},{3,2},{4,5},{5,4},{6,7},{7,6},{8,9},{9,8},{10,11... | collective-permute-start | bytes 786440 | tf_op jit(solution)/shard_map/ppermute | solution.py:345
  9.6 0.2 copy.22
  9.8 0.1 collective-permute-start.6
  9.9 0.0 copy-done.2
  10.0 0.1 stack.12
  10.0 0.1 copy.5
  10.1 0.1 stack.13
  10.2 0.1 copy.6
  10.3 0.1 stack.14
  10.4 0.1 copy.7
  10.4 0.0 copy-done.1
  10.4 0.7 copy.20
  11.1 0.0 copy-done
  11.1 0.7 copy.21
  11.8 1.4 collective-permute-done
  13.2 4.0 %collective-permute-start.1 = (bf16[8,16384]{1,0:T(8,128)(2,1)S(1)}, bf16[8,16384]{1,0:T(8,128)(2,1)S(1)}, u32[]{:S(2)}, u32[]{:S(2)}) collective-permute-start(bf16[8,16384]{1,0:T(8,128)(2,1)S(1)} %collective-permute-done), channel_id=1, source_target_pairs={{0,2},{2,4},{4,6},{3,1},{5,3},{7,5},{8,10},{10,12},{12,14},{11,9},... | collective-permute-start | bytes 786440 | tf_op jit(solution)/shard_map/ppermute | solution.py:347
  17.3 1.6 %collective-permute-done.2 = bf16[8,16384]{1,0:T(8,128)(2,1)S(1)} collective-permute-done((bf16[8,16384]{1,0:T(8,128)(2,1)}, bf16[8,16384]{1,0:T(8,128)(2,1)S(1)}, u32[]{:S(2)}, u32[]{:S(2)}) %collective-permute-start.2) | collective-permute-done | bytes 262176 | tf_op jit(solution)/shard_map/ppermute | solution.py:345
  18.9 4.0 %collective-permute-start.3 = (bf16[8,16384]{1,0:T(8,128)(2,1)S(1)}, bf16[8,16384]{1,0:T(8,128)(2,1)S(1)}, u32[]{:S(2)}, u32[]{:S(2)}) collective-permute-start(bf16[8,16384]{1,0:T(8,128)(2,1)S(1)} %collective-permute-done.2), channel_id=1, source_target_pairs={{0,2},{2,4},{4,6},{3,1},{5,3},{7,5},{8,10},{10,12},{12,14},{11,9},... | collective-permute-start | bytes 786440 | tf_op jit(solution)/shard_map/ppermute | solution.py:347
  22.9 1.6 %collective-permute-done.4 = bf16[8,16384]{1,0:T(8,128)(2,1)S(1)} collective-permute-done((bf16[8,16384]{1,0:T(8,128)(2,1)}, bf16[8,16384]{1,0:T(8,128)(2,1)S(1)}, u32[]{:S(2)}, u32[]{:S(2)}) %collective-permute-start.4) | collective-permute-done | bytes 262176 | tf_op jit(solution)/shard_map/ppermute | solution.py:345
  24.5 4.0 %collective-permute-start.5 = (bf16[8,16384]{1,0:T(8,128)(2,1)S(1)}, bf16[8,16384]{1,0:T(8,128)(2,1)S(1)}, u32[]{:S(2)}, u32[]{:S(2)}) collective-permute-start(bf16[8,16384]{1,0:T(8,128)(2,1)S(1)} %collective-permute-done.4), channel_id=1, source_target_pairs={{0,2},{2,4},{4,6},{3,1},{5,3},{7,5},{8,10},{10,12},{12,14},{11,9},... | collective-permute-start | bytes 786440 | tf_op jit(solution)/shard_map/ppermute | solution.py:347
  28.5 0.7 collective-permute-done.6
  29.2 3.7 %collective-permute-start.7 = (bf16[8,16384]{1,0:T(8,128)(2,1)S(1)}, bf16[8,16384]{1,0:T(8,128)(2,1)S(1)}, u32[]{:S(2)}, u32[]{:S(2)}) collective-permute-start(bf16[8,16384]{1,0:T(8,128)(2,1)S(1)} %collective-permute-done.6), channel_id=1, source_target_pairs={{0,2},{2,4},{4,6},{3,1},{5,3},{7,5},{8,10},{10,12},{12,14},{11,9},... | collective-permute-start | bytes 786440 | tf_op jit(solution)/shard_map/ppermute | solution.py:347
  33.1 0.0 collective-permute-done.1
  33.1 0.0 collective-permute-done.3
  33.1 0.0 collective-permute-done.5
  33.2 4.8 %collective-permute-done.7 = bf16[8,16384]{1,0:T(8,128)(2,1)S(1)} collective-permute-done((bf16[8,16384]{1,0:T(8,128)(2,1)S(1)}, bf16[8,16384]{1,0:T(8,128)(2,1)S(1)}, u32[]{:S(2)}, u32[]{:S(2)}) %collective-permute-start.7) | collective-permute-done | bytes 262176 | tf_op jit(solution)/shard_map/ppermute | solution.py:347
  38.0 0.1 broadcast_select_fusion
  38.2 4.5 %local_sums.1 = f32[28,128,128]{2,1,0:T(8,128)S(1)} custom-call(bf16[32,16384]{1,0:T(8,128)(2,1)S(1)} %bitcast.42, bf16[32,16384]{1,0:T(8,128)(2,1)S(1)} %get-tuple-element.6.before, bf16[32,16384]{1,0:T(8,128)(2,1)S(1)} %get-tuple-element.5.after, bf16[32,16384]{1,0:T(8,128)(2,1)S(1)} %bitcast.41, s32[96,16]{1,0:T(8,128)S(1)} %bitcast.43), custom_call_target="tpu_custom_call" | custom-call | tf_op jit(solution)/shard_map/local_sums/pallas_call | solution.py:376
  42.6 41.9 %sum_everywhere.1 = f32[3584,128]{1,0:T(8,128)S(1)} custom-call(f32[3584,128]{1,0:T(8,128)S(1)} %bitcast.40), custom_call_target="tpu_custom_call" | custom-call | tf_op jit(solution)/shard_map/sum_everywhere/pallas_call | solution.py:324
  84.6 65.9 %solve.1 = (f32[32,864]{1,0:T(8,128)}, f32[32,864]{1,0:T(8,128)}) custom-call(f32[28,128,128]{2,1,0:T(8,128)S(1)} %bitcast.39), custom_call_target="tpu_custom_call" | custom-call | tf_op jit(solution)/shard_map/solve/pallas_call | solution.py:391
  (10 shorter events, 0.2 us)
Async XLA Ops:
  0.6 9.3 %copy-start.2 = (s32[1,512]{1,0:T(1,128)S(1)}, s32[1,512]{1,0:T(1,128)}, u32[]{:S(2)}) copy-start(s32[1,512]{1,0:T(1,128)} %param.5) | copy-start | bytes 6148
  0.6 9.8 %copy-start.1 = (bf16[1,32,1,128,128]{4,3,2,1,0:T(8,128)(2,1)S(1)}, bf16[1,32,1,128,128]{4,3,2,1,0:T(8,128)(2,1)}, u32[]{:S(2)}) copy-start(bf16[1,32,1,128,128]{4,3,2,1,0:T(8,128)(2,1)} %param.4) | copy-start | bytes 3145732
  2.9 10.3 %collective-permute-start = (bf16[8,16384]{1,0:T(8,128)(2,1)}, bf16[8,16384]{1,0:T(8,128)(2,1)S(1)}, u32[]{:S(2)}, u32[]{:S(2)}) collective-permute-start(bf16[8,16384]{1,0:T(8,128)(2,1)} %bitcast.38), channel_id=1, source_target_pairs={{0,1},{1,0},{2,3},{3,2},{4,5},{5,4},{6,7},{7,6},{8,9},{9,8},{10,11... | collective-permute-start | bytes 786440 | tf_op jit(solution)/shard_map/ppermute | solution.py:345
  5.9 5.2 %copy-start = (bf16[1,32,1,128,128]{4,3,2,1,0:T(8,128)(2,1)S(1)}, bf16[1,32,1,128,128]{4,3,2,1,0:T(8,128)(2,1)}, u32[]{:S(2)}) copy-start(bf16[1,32,1,128,128]{4,3,2,1,0:T(8,128)(2,1)} %param.3) | copy-start | bytes 3145732
  6.8 12.1 %collective-permute-start.2 = (bf16[8,16384]{1,0:T(8,128)(2,1)}, bf16[8,16384]{1,0:T(8,128)(2,1)S(1)}, u32[]{:S(2)}, u32[]{:S(2)}) collective-permute-start(bf16[8,16384]{1,0:T(8,128)(2,1)} %bitcast.37), channel_id=1, source_target_pairs={{0,1},{1,0},{2,3},{3,2},{4,5},{5,4},{6,7},{7,6},{8,9},{9,8},{10,11... | collective-permute-start | bytes 786440 | tf_op jit(solution)/shard_map/ppermute | solution.py:345
  7.6 16.9 %collective-permute-start.4 = (bf16[8,16384]{1,0:T(8,128)(2,1)}, bf16[8,16384]{1,0:T(8,128)(2,1)S(1)}, u32[]{:S(2)}, u32[]{:S(2)}) collective-permute-start(bf16[8,16384]{1,0:T(8,128)(2,1)} %bitcast.36), channel_id=1, source_target_pairs={{0,1},{1,0},{2,3},{3,2},{4,5},{5,4},{6,7},{7,6},{8,9},{9,8},{10,11... | collective-permute-start | bytes 786440 | tf_op jit(solution)/shard_map/ppermute | solution.py:345
  9.8 19.4 %collective-permute-start.6 = (bf16[8,16384]{1,0:T(8,128)(2,1)S(1)}, bf16[8,16384]{1,0:T(8,128)(2,1)S(1)}, u32[]{:S(2)}, u32[]{:S(2)}) collective-permute-start(bf16[8,16384]{1,0:T(8,128)(2,1)S(1)} %bitcast.46), channel_id=1, source_target_pairs={{0,1},{1,0},{2,3},{3,2},{4,5},{5,4},{6,7},{7,6},{8,9},{9,8},{10,11... | collective-permute-start | bytes 786440 | tf_op jit(solution)/shard_map/ppermute | solution.py:345
  13.2 19.8 %collective-permute-start.1 = (bf16[8,16384]{1,0:T(8,128)(2,1)S(1)}, bf16[8,16384]{1,0:T(8,128)(2,1)S(1)}, u32[]{:S(2)}, u32[]{:S(2)}) collective-permute-start(bf16[8,16384]{1,0:T(8,128)(2,1)S(1)} %collective-permute-done), channel_id=1, source_target_pairs={{0,2},{2,4},{4,6},{3,1},{5,3},{7,5},{8,10},{10,12},{12,14},{11,9},... | collective-permute-start | bytes 786440 | tf_op jit(solution)/shard_map/ppermute | solution.py:347
  18.9 14.3 %collective-permute-start.3 = (bf16[8,16384]{1,0:T(8,128)(2,1)S(1)}, bf16[8,16384]{1,0:T(8,128)(2,1)S(1)}, u32[]{:S(2)}, u32[]{:S(2)}) collective-permute-start(bf16[8,16384]{1,0:T(8,128)(2,1)S(1)} %collective-permute-done.2), channel_id=1, source_target_pairs={{0,2},{2,4},{4,6},{3,1},{5,3},{7,5},{8,10},{10,12},{12,14},{11,9},... | collective-permute-start | bytes 786440 | tf_op jit(solution)/shard_map/ppermute | solution.py:347
  24.5 8.7 %collective-permute-start.5 = (bf16[8,16384]{1,0:T(8,128)(2,1)S(1)}, bf16[8,16384]{1,0:T(8,128)(2,1)S(1)}, u32[]{:S(2)}, u32[]{:S(2)}) collective-permute-start(bf16[8,16384]{1,0:T(8,128)(2,1)S(1)} %collective-permute-done.4), channel_id=1, source_target_pairs={{0,2},{2,4},{4,6},{3,1},{5,3},{7,5},{8,10},{10,12},{12,14},{11,9},... | collective-permute-start | bytes 786440 | tf_op jit(solution)/shard_map/ppermute | solution.py:347
  29.2 8.7 %collective-permute-start.7 = (bf16[8,16384]{1,0:T(8,128)(2,1)S(1)}, bf16[8,16384]{1,0:T(8,128)(2,1)S(1)}, u32[]{:S(2)}, u32[]{:S(2)}) collective-permute-start(bf16[8,16384]{1,0:T(8,128)(2,1)S(1)} %collective-permute-done.6), channel_id=1, source_target_pairs={{0,2},{2,4},{4,6},{3,1},{5,3},{7,5},{8,10},{10,12},{12,14},{11,9},... | collective-permute-start | bytes 786440 | tf_op jit(solution)/shard_map/ppermute | solution.py:347

commit v3 on v2

--- a/solution.py
+++ b/solution.py
@@ -17,15 +17,27 @@
 NT = (((1,), (1,)), ((), ()))
 
 
-def local_kernel(width, own, before, after, grads, targets, out, apad, samples, wsum):
+def local_kernel(width, own, swapped, relayed, grads, targets, out, apad, samples, wsum):
     channels, cells = own.shape
     outputs = grads.shape[0]
     per_chunk = targets.shape[0] // 3
     rows = 27 * channels
     total = samples.shape[0]
     third = 9 * channels
-    for a, plane in enumerate((before, own, after)):
-        apad[a * channels : (a + 1) * channels, width : width + cells] = plane[...]
+    odd = lax.axis_index("slab") % 2 == 1
+    inner = slice(width, width + cells)
+    apad[channels : 2 * channels, inner] = own[...]
+
+    @pl.when(odd)
+    def _():
+        apad[:channels, inner] = swapped[...]
+        apad[2 * channels :, inner] = relayed[...]
+
+    @pl.when(jnp.logical_not(odd))
+    def _():
+        apad[:channels, inner] = relayed[...]
+        apad[2 * channels :, inner] = swapped[...]
+
     apad[:, 0:width] = jnp.zeros((3 * channels, width), apad.dtype)
     apad[:, width + cells :] = jnp.zeros((3 * channels, width), apad.dtype)
     lane = lax.broadcasted_iota(jnp.int32, (outputs, CHUNK), 1) % width
@@ -140,18 +152,16 @@
     factor = total[slots[count - 1, count - 1]][offset:, offset:] / sample_total
     factor = jnp.where(gr == gc, factor + shift_g, factor)
 
-    def eliminate(k, m):
-        row = jnp.sum(jnp.where(gr == k, m, 0.0), axis=0, keepdims=True)
-        col = jnp.sum(jnp.where(gc == k, m, 0.0), axis=1, keepdims=True)
-        pivot = jnp.sum(jnp.where(gr[:, :1] == k, col, 0.0), axis=0, keepdims=True)
-        inverse = 1.0 / pivot
+    inverse_g = factor
+    for k in range(outputs):
+        row = inverse_g[k : k + 1, :]
+        col = inverse_g[:, k : k + 1]
+        inverse = 1.0 / inverse_g[k : k + 1, k : k + 1]
         scaled = row * inverse
-        rest = m - col * scaled
+        rest = inverse_g - col * scaled
         rest = jnp.where(gr == k, scaled, rest)
         rest = jnp.where(gc == k, -col * inverse, rest)
-        return jnp.where((gr == k) & (gc == k), inverse, rest)
-
-    inverse_g = lax.fori_loop(0, outputs, eliminate, factor)
+        inverse_g = jnp.where((gr == k) & (gc == k), inverse, rest)
     weights = w_ref[...]
     rhs = jnp.dot(
         weights, inverse_g, precision=lax.Precision.HIGHEST, preferred_element_type=jnp.float32
@@ -164,7 +174,7 @@
     z = residual * inv_ref[...]
     p_ref[...] = z
     rz0 = jnp.sum(residual * z, axis=0, keepdims=True)
-    goal = rz0 * 1e-16
+    goal = rz0 * 1e-13
 
     def unfinished(state):
         step, rz = state
@@ -336,19 +346,79 @@
     )(value)
 
 
+def halo_kernel(size, parts, own, swapped, relayed, send_sem, recv_sem):
+    dp, me = lax.axis_index("dp"), lax.axis_index("slab")
+    odd = me % 2
+    mate = me + 1 - 2 * odd
+    target = me + 2 - 4 * odd
+    source = me - 2 + 4 * odd
+    gives = (target >= 0) & (target < size)
+    takes = (source >= 0) & (source < size)
+    barrier = pltpu.get_barrier_semaphore()
+    pl.semaphore_signal(barrier, inc=1, device_id=(dp, mate), device_id_type=MESH)
+
+    @pl.when(gives)
+    def _():
+        pl.semaphore_signal(barrier, inc=1, device_id=(dp, target), device_id_type=MESH)
+
+    @pl.when(takes)
+    def _():
+        pl.semaphore_signal(barrier, inc=1, device_id=(dp, source), device_id_type=MESH)
+
+    pl.semaphore_wait(barrier, 1 + gives.astype(jnp.int32) + takes.astype(jnp.int32))
+    step = own.shape[1] // parts
+
+    def piece(kind, n):
+        here = slice(n * step, (n + 1) * step)
+        return pltpu.make_async_remote_copy(
+            src_ref=(own if kind == 0 else swapped).at[:, here],
+            dst_ref=(swapped if kind == 0 else relayed).at[:, here],
+            send_sem=send_sem.at[kind, n],
+            recv_sem=recv_sem.at[kind, n],
+            device_id=(dp, mate if kind == 0 else target),
+            device_id_type=MESH,
+        )
+
+    for n in range(parts):
+        piece(0, n).start()
+
+    @pl.when(jnp.logical_not(takes))
+    def _():
+        relayed[...] = jnp.zeros_like(relayed)
+
+    for n in range(parts):
+        piece(0, n).wait_recv()
+
+        @pl.when(gives)
+        def _():
+            piece(1, n).start()
+
+    for n in range(parts):
+        piece(0, n).wait_send()
+
+        @pl.when(gives)
+        def _():
+            piece(1, n).wait_send()
+
+        @pl.when(takes)
+        def _():
+            piece(1, n).wait_recv()
+
+
 def halo(plane):
-    size = lax.axis_size("slab")
-    pairs = [(i, i ^ 1) for i in range(size) if i ^ 1 < size]
-    relays = [(i, i + 2) for i in range(0, size - 2, 2)] + [(i, i - 2) for i in range(3, size, 2)]
-    swapped, relayed = [], []
-    for part in jnp.split(plane, 4, axis=0):
-        got = lax.ppermute(part, "slab", pairs)
-        swapped.append(got)
-        relayed.append(lax.ppermute(got, "slab", relays))
-    swapped = jnp.concatenate(swapped, axis=0)
-    relayed = jnp.concatenate(relayed, axis=0)
-    even = lax.axis_index("slab") % 2 == 0
-    return jnp.where(even, relayed, swapped), jnp.where(even, swapped, relayed)
+    size, parts = lax.axis_size("slab"), 8
+    swapped, relayed = pl.pallas_call(
+        functools.partial(halo_kernel, size, parts),
+        out_shape=[jax.ShapeDtypeStruct(plane.shape, plane.dtype)] * 2,
+        in_specs=[pl.BlockSpec(memory_space=pltpu.VMEM)],
+        out_specs=[pl.BlockSpec(memory_space=pltpu.VMEM)] * 2,
+        scratch_shapes=[pltpu.SemaphoreType.DMA((2, parts))] * 2,
+        compiler_params=pltpu.CompilerParams(
+            collective_id=1, has_side_effects=True, vmem_limit_bytes=16 * 1024 * 1024
+        ),
+        name="halo",
+    )(plane)
+    return swapped, relayed
 
 
 def shards(acts, grads, picks):
@@ -357,7 +427,7 @@
     cells = height * width
     own = acts.reshape(channels, cells)
     rows = grads.reshape(outputs, cells)
-    before, after = halo(own)
+    swapped, relayed = halo(own)
     samples = picks.shape[1]
     chunks = cells // CHUNK
     position = jnp.arange(samples, dtype=jnp.int32) * 32 + picks.reshape(samples)
@@ -385,7 +455,7 @@
         ],
         compiler_params=pltpu.CompilerParams(vmem_limit_bytes=48 * 1024 * 1024),
         name="local_sums",
-    )(own, before, after, rows, targets)
+    )(own, swapped, relayed, rows, targets)
     total = sum_everywhere(partial.reshape(-1, BLOCK)).reshape(partial.shape)
     everyone = lax.axis_size("dp") * lax.axis_size("slab") * volumes
     return pl.pallas_call(

time: 148 us -> 137 us (0.926)
  Pallas kernels: 112 us -> 134 us
  starting transfers between devices: 20.9 us -> 0 us
  waiting for transfers between devices: 10.1 us -> 0 us
  local copies, waits for them, and re-layouts: 6.15 us -> 3.3 us
    pallas_call x0 -> x1, Pallas kernels: none -> 31.3 us  [halo(): pl.pallas_call(functools.partial(halo_kernel, size, parts), out_shape=[ja...]
    ppermute x8 -> x0, starting transfers between devices: 20.9 us -> none  [the longest x4 15.8 us: halo(): relayed.append(lax.ppermute(got, 'slab', relays))]
    ppermute x8 -> x0, waiting for transfers between devices: 10.1 us -> none  [the longest x4 5.3 us: halo(): got = lax.ppermute(part, 'slab', pairs)]
    pallas_call x1, Pallas kernels: 65.9 us -> 56.5 us  [shards(): pl.pallas_call(functools.partial(solve_kernel, everyone * planes * cells,...]
    unnamed x19 -> x0, local copies, waits for them, and re-layouts: 5.66 us -> none
    reshape x0 -> x1, local copies, waits for them, and re-layouts: none -> 2.84 us  [shards(): rows = grads.reshape(outputs, cells)]
  transfers between devices with their start and end apart: 8 -> 0, of which waited for: 5 -> 0; matrix products, arithmetic and copies ran while one was open for 3% -> 0% of each run, Pallas kernels for 0% -> 0%
where the time goes in v3:
time: 137 us; the launch traced here: 139 us
  Pallas kernels  134 us (98%)
  local copies, waits for them, and re-layouts  3.3 us (2%)
    pallas_call x1, Pallas kernels, shards(): pl.pallas_call(functools.partial(solve_kernel, everyone * planes * cells,...  56.5 us
    pallas_call x1, Pallas kernels, sum_everywhere(): pl.pallas_call(functools.partial(sum_kernel, plan), out_shape=jax.ShapeDt...  41.8 us
    pallas_call x1, Pallas kernels, halo(): pl.pallas_call(functools.partial(halo_kernel, size, parts), out_shape=[ja...  31.3 us
    pallas_call x1, Pallas kernels, shards(): pl.pallas_call(functools.partial(local_kernel, width), out_shape=jax.Shap...  4.63 us
    reshape x1, local copies, waits for them, and re-layouts, shards(): rows = grads.reshape(outputs, cells)  2.84 us

profile of v3, /device:TPU:0, one launch (start us, length us, event | category | flops | bytes accessed | tf_op | source)
XLA Modules:
  0.0 139.0 jit_solution(5639692708123113452)
XLA Ops:
  0.6 0.7 fusion.1
  1.4 0.1 stack.12
  1.4 0.1 copy.5
  1.5 0.1 stack.13
  1.6 0.1 copy.6
  1.7 0.1 stack.14
  1.7 0.1 copy.7
  1.8 2.8 %copy_bitcast_fusion = (bf16[32,16384]{1,0:T(8,128)(2,1)S(1)}, bf16[32,16384]{1,0:T(8,128)(2,1)S(1)}) fusion(bf16[4,8,128,128]{3,2,1,0:T(8,128)(2,1)} %bitcast.16, bf16[4,8,128,128]{3,2,1,0:T(8,128)(2,1)} %bitcast.17), kind=kLoop, calls=%fused_computation | loop fusion | bytes 4194304 | tf_op jit(solution)/shard_map/reshape | solution.py:429
  4.7 31.3 %halo.1 = (bf16[32,16384]{1,0:T(8,128)(2,1)S(1)}, bf16[32,16384]{1,0:T(8,128)(2,1)S(1)}) custom-call(bf16[32,16384]{1,0:T(8,128)(2,1)S(1)} %get-tuple-element.10.own), custom_call_target="tpu_custom_call" | custom-call | tf_op jit(solution)/shard_map/halo/pallas_call | solution.py:410
  36.0 4.6 %local_sums.1 = f32[28,128,128]{2,1,0:T(8,128)S(1)} custom-call(bf16[32,16384]{1,0:T(8,128)(2,1)S(1)} %get-tuple-element.10.own, bf16[32,16384]{1,0:T(8,128)(2,1)S(1)} %get-tuple-element.4.swapped, bf16[32,16384]{1,0:T(8,128)(2,1)S(1)} %get-tuple-element.5.relayed, bf16[32,16384]{1,0:T(8,128)(2,1)S(1)} %get-tuple-element.9.grads, s32[96,16]{1,0:T(8,128)S(1)} %bitcast.15), custom_call_target="tpu_custom_call" | custom-call | tf_op jit(solution)/shard_map/local_sums/pallas_call | solution.py:446
  40.7 41.8 %sum_everywhere.1 = f32[3584,128]{1,0:T(8,128)S(1)} custom-call(f32[3584,128]{1,0:T(8,128)S(1)} %bitcast.14), custom_call_target="tpu_custom_call" | custom-call | tf_op jit(solution)/shard_map/sum_everywhere/pallas_call | solution.py:334
  82.5 56.5 %solve.1 = (f32[32,864]{1,0:T(8,128)}, f32[32,864]{1,0:T(8,128)}) custom-call(f32[28,128,128]{2,1,0:T(8,128)S(1)} %bitcast.13), custom_call_target="tpu_custom_call" | custom-call | tf_op jit(solution)/shard_map/solve/pallas_call | solution.py:461
  (1 shorter events, 0.0 us)

commit v4 on v3

--- a/solution.py
+++ b/solution.py
@@ -233,7 +233,8 @@
 
 def portion_plan(rows, orders):
     unit = rows // 14
-    sizes = [5 * unit, 5 * unit, rows - 10 * unit]
+    sizes = [3 * unit, 3 * unit, 2 * unit, 2 * unit, 2 * unit, rows - 12 * unit]
+    orders = orders + orders
     plan, start = [], 0
     for size, order in zip(sizes, orders):
         stages, length = [], size

time: 137 us -> 135 us (0.985)
  Pallas kernels: 134 us -> 131 us
    pallas_call x1, Pallas kernels: 41.8 us -> 38.8 us  [sum_everywhere(): pl.pallas_call(functools.partial(sum_kernel, plan), out_shape=jax.ShapeDt...]
where the time goes in v4:
time: 135 us; the launch traced here: 136 us
  Pallas kernels  131 us (97%)
  local copies, waits for them, and re-layouts  3.3 us (2%)
    pallas_call x1, Pallas kernels, shards(): pl.pallas_call(functools.partial(solve_kernel, everyone * planes * cells,...  56.5 us
    pallas_call x1, Pallas kernels, sum_everywhere(): pl.pallas_call(functools.partial(sum_kernel, plan), out_shape=jax.ShapeDt...  38.8 us
    pallas_call x1, Pallas kernels, halo(): pl.pallas_call(functools.partial(halo_kernel, size, parts), out_shape=[ja...  31.3 us
    pallas_call x1, Pallas kernels, shards(): pl.pallas_call(functools.partial(local_kernel, width), out_shape=jax.Shap...  4.63 us
    reshape x1, local copies, waits for them, and re-layouts, shards(): rows = grads.reshape(outputs, cells)  2.84 us

profile of v4, /device:TPU:0, one launch (start us, length us, event | category | flops | bytes accessed | tf_op | source)
XLA Modules:
  0.0 135.9 jit_solution(15656885913746863020)
XLA Ops:
  0.6 0.7 fusion.1
  1.4 0.1 stack.12
  1.4 0.1 copy.5
  1.5 0.1 stack.13
  1.6 0.1 copy.6
  1.7 0.1 stack.14
  1.7 0.1 copy.7
  1.8 2.8 %copy_bitcast_fusion = (bf16[32,16384]{1,0:T(8,128)(2,1)S(1)}, bf16[32,16384]{1,0:T(8,128)(2,1)S(1)}) fusion(bf16[4,8,128,128]{3,2,1,0:T(8,128)(2,1)} %bitcast.16, bf16[4,8,128,128]{3,2,1,0:T(8,128)(2,1)} %bitcast.17), kind=kLoop, calls=%fused_computation | loop fusion | bytes 4194304 | tf_op jit(solution)/shard_map/reshape | solution.py:430
  4.7 31.3 %halo.1 = (bf16[32,16384]{1,0:T(8,128)(2,1)S(1)}, bf16[32,16384]{1,0:T(8,128)(2,1)S(1)}) custom-call(bf16[32,16384]{1,0:T(8,128)(2,1)S(1)} %get-tuple-element.10.own), custom_call_target="tpu_custom_call" | custom-call | tf_op jit(solution)/shard_map/halo/pallas_call | solution.py:411
  36.0 4.6 %local_sums.1 = f32[28,128,128]{2,1,0:T(8,128)S(1)} custom-call(bf16[32,16384]{1,0:T(8,128)(2,1)S(1)} %get-tuple-element.10.own, bf16[32,16384]{1,0:T(8,128)(2,1)S(1)} %get-tuple-element.4.swapped, bf16[32,16384]{1,0:T(8,128)(2,1)S(1)} %get-tuple-element.5.relayed, bf16[32,16384]{1,0:T(8,128)(2,1)S(1)} %get-tuple-element.9.grads, s32[96,16]{1,0:T(8,128)S(1)} %bitcast.15), custom_call_target="tpu_custom_call" | custom-call | tf_op jit(solution)/shard_map/local_sums/pallas_call | solution.py:447
  40.7 38.8 %sum_everywhere.1 = f32[3584,128]{1,0:T(8,128)S(1)} custom-call(f32[3584,128]{1,0:T(8,128)S(1)} %bitcast.14), custom_call_target="tpu_custom_call" | custom-call | tf_op jit(solution)/shard_map/sum_everywhere/pallas_call | solution.py:335
  79.4 56.5 %solve.1 = (f32[32,864]{1,0:T(8,128)}, f32[32,864]{1,0:T(8,128)}) custom-call(f32[28,128,128]{2,1,0:T(8,128)S(1)} %bitcast.13), custom_call_target="tpu_custom_call" | custom-call | tf_op jit(solution)/shard_map/solve/pallas_call | solution.py:462
  (1 shorter events, 0.0 us)

commit v5 on v4

--- a/solution.py
+++ b/solution.py
@@ -407,7 +407,7 @@
 
 
 def halo(plane):
-    size, parts = lax.axis_size("slab"), 8
+    size, parts = lax.axis_size("slab"), 16
     swapped, relayed = pl.pallas_call(
         functools.partial(halo_kernel, size, parts),
         out_shape=[jax.ShapeDtypeStruct(plane.shape, plane.dtype)] * 2,

time: 135 us -> 134 us (level); the launches traced: 136 us -> 133 us
  Pallas kernels: 131 us -> 128 us
    pallas_call x1, Pallas kernels: 56.5 us -> 54.3 us  [shards(): pl.pallas_call(functools.partial(solve_kernel, everyone * planes * cells,...]
where the time goes in v5:
time: 134 us; the launch traced here: 133 us
  Pallas kernels  128 us (96%)
  local copies, waits for them, and re-layouts  3.3 us (2%)
    pallas_call x1, Pallas kernels, shards(): pl.pallas_call(functools.partial(solve_kernel, everyone * planes * cells,...  54.3 us
    pallas_call x1, Pallas kernels, sum_everywhere(): pl.pallas_call(functools.partial(sum_kernel, plan), out_shape=jax.ShapeDt...  38.8 us
    pallas_call x1, Pallas kernels, halo(): pl.pallas_call(functools.partial(halo_kernel, size, parts), out_shape=[ja...  30.2 us
    pallas_call x1, Pallas kernels, shards(): pl.pallas_call(functools.partial(local_kernel, width), out_shape=jax.Shap...  4.63 us
    reshape x1, local copies, waits for them, and re-layouts, shards(): rows = grads.reshape(outputs, cells)  2.84 us

profile of v5, /device:TPU:0, one launch (start us, length us, event | category | flops | bytes accessed | tf_op | source)
XLA Modules:
  0.0 132.6 jit_solution(11114071978819816725)
XLA Ops:
  0.6 0.7 fusion.1
  1.4 0.1 stack.12
  1.4 0.1 copy.5
  1.5 0.1 stack.13
  1.6 0.1 copy.6
  1.7 0.1 stack.14
  1.7 0.1 copy.7
  1.8 2.8 %copy_bitcast_fusion = (bf16[32,16384]{1,0:T(8,128)(2,1)S(1)}, bf16[32,16384]{1,0:T(8,128)(2,1)S(1)}) fusion(bf16[4,8,128,128]{3,2,1,0:T(8,128)(2,1)} %bitcast.16, bf16[4,8,128,128]{3,2,1,0:T(8,128)(2,1)} %bitcast.17), kind=kLoop, calls=%fused_computation | loop fusion | bytes 4194304 | tf_op jit(solution)/shard_map/reshape | solution.py:430
  4.7 30.2 %halo.1 = (bf16[32,16384]{1,0:T(8,128)(2,1)S(1)}, bf16[32,16384]{1,0:T(8,128)(2,1)S(1)}) custom-call(bf16[32,16384]{1,0:T(8,128)(2,1)S(1)} %get-tuple-element.10.own), custom_call_target="tpu_custom_call" | custom-call | tf_op jit(solution)/shard_map/halo/pallas_call | solution.py:411
  34.9 4.6 %local_sums.1 = f32[28,128,128]{2,1,0:T(8,128)S(1)} custom-call(bf16[32,16384]{1,0:T(8,128)(2,1)S(1)} %get-tuple-element.10.own, bf16[32,16384]{1,0:T(8,128)(2,1)S(1)} %get-tuple-element.4.swapped, bf16[32,16384]{1,0:T(8,128)(2,1)S(1)} %get-tuple-element.5.relayed, bf16[32,16384]{1,0:T(8,128)(2,1)S(1)} %get-tuple-element.9.grads, s32[96,16]{1,0:T(8,128)S(1)} %bitcast.15), custom_call_target="tpu_custom_call" | custom-call | tf_op jit(solution)/shard_map/local_sums/pallas_call | solution.py:447
  39.5 38.8 %sum_everywhere.1 = f32[3584,128]{1,0:T(8,128)S(1)} custom-call(f32[3584,128]{1,0:T(8,128)S(1)} %bitcast.14), custom_call_target="tpu_custom_call" | custom-call | tf_op jit(solution)/shard_map/sum_everywhere/pallas_call | solution.py:335
  78.3 54.3 %solve.1 = (f32[32,864]{1,0:T(8,128)}, f32[32,864]{1,0:T(8,128)}) custom-call(f32[28,128,128]{2,1,0:T(8,128)S(1)} %bitcast.13), custom_call_target="tpu_custom_call" | custom-call | tf_op jit(solution)/shard_map/solve/pallas_call | solution.py:462
  (1 shorter events, 0.0 us)
